TPU v7x, 32 devices: a whole 2x2x4 slice. The times are simulated.
32 devices in a mesh: tm: 4 (over x, core), anta: 4 (over z), antb: 2 (over y).
Axes of the slice: x: 2, y: 2, z: 4, core: 2. Of those that a mesh axis runs over, the one named last changes fastest.
Arguments:
- samples: bfloat16 [2, 512, 6144], P('antb', 'anta', 'tm'), may hold values from -6 to 6
Outputs:
- correlation: float32 [256, 2, 512, 2, 512], P('tm', None, 'anta', 'antb')
All inputs are finite; a program needn't handle non-finite values.
Results may differ from a plain program's by a relative error of at most 0.0003.
Values may be sent and summed in bfloat16 or wider, within the bound.
A program may use at most 128 MiB of HBM per device.

v0:
```python
import math
import jax
import jax.numpy as jnp
from jax import lax
from jax.sharding import PartitionSpec as P

ANTENNA_COUNT = 512
POLARISATION_NUM = 2
LAG_TOTAL = 256


def lag_terms(row_padded, columns, lag_start, lag_count, window_len):
    group_len = math.gcd(lag_count, 8)
    flat_cols = columns.reshape(columns.shape[1], columns.shape[2])

    def one_group(group_index):
        first_lag = lag_start + group_index * group_len
        pieces = [
            lax.dynamic_slice_in_dim(row_padded, LAG_TOTAL - first_lag - step_index, window_len, 1)
            for step_index in range(group_len)
        ]
        stacked = jnp.stack(pieces, 0)
        return jnp.einsum("kit,jt->kij", stacked, flat_cols, preferred_element_type=jnp.float32)

    grouped = lax.map(one_group, jnp.arange(lag_count // group_len, dtype=jnp.int32))
    return grouped.reshape(lag_count, row_padded.shape[0], flat_cols.shape[0])


def collect_rows(own_window):
    return lax.all_gather(own_window, "antb", axis=0, tiled=True)


def per_device(samples):
    antenna_total = samples.shape[1]
    block_len = samples.shape[2]
    tm_size = lax.axis_size("tm")
    lag_portion = LAG_TOTAL // tm_size
    full_length = block_len * tm_size
    factor = 1.0 / math.sqrt(full_length)
    lag_start = lax.axis_index("tm") * lag_portion
    col_tiles = lax.all_gather(samples, "anta", axis=1, tiled=True)
    columns = lax.all_gather(col_tiles, "tm", axis=2, tiled=True)
    own_rows = lax.dynamic_slice_in_dim(
        columns, lax.axis_index("anta") * antenna_total, antenna_total, 1
    )
    row_samples = collect_rows(own_rows)
    row_padded = jnp.pad(
        row_samples.reshape(POLARISATION_NUM * antenna_total, full_length), ((0, 0), (LAG_TOTAL, 0))
    )
    lag_group_block = lag_terms(row_padded, columns, lag_start, lag_portion, full_length)
    accumulated_sum = lag_group_block.reshape(
        lag_portion, POLARISATION_NUM, antenna_total, 1, ANTENNA_COUNT
    )
    return accumulated_sum * factor


def solution(mesh):
    return jax.shard_map(
        per_device,
        mesh=mesh,
        in_specs=(P("antb", "anta", "tm"),),
        out_specs=P("tm", None, "anta", "antb", None),
        check_vma=False,
    )
```

profile of v0, /device:TPU:0, one launch (start us, length us, event | category | flops | bytes accessed | tf_op | source)
XLA Modules:
  0.0 584.9 jit_solution(11511170079034413192)
XLA Ops:
  7.3 41.4 %all-gather.4.cloned.1.call-done = bf16[1,512,1536]{2,1,0:T(8,128)(2,1)} async-done(((bf16[1,128,1536]{2,1,0:T(8,128)(2,1)}), bf16[1,512,1536]{2,1,0:T(8,128)(2,1)}) %all-gather.4.cloned.1.call-update) | async-done | bytes 1572880 | tf_op jit(solution)/shard_map/all_gather | solution.py:41
  48.8 46.7 %all-gather.6.cloned.1.call-done = bf16[1,512,6144]{2,1,0:T(8,128)(2,1)} async-done(((bf16[1,512,1536]{2,1,0:T(8,128)(2,1)}), bf16[1,512,6144]{2,1,0:T(8,128)(2,1)}) %all-gather.6.cloned.1.call-update) | async-done | bytes 6291472 | tf_op jit(solution)/shard_map/all_gather | solution.py:42
  98.2 45.1 %all-gather.8.cloned.1.call-done = bf16[2,128,6144]{2,1,0:T(8,128)(2,1)} async-done(((bf16[1,128,6144]{2,1,0:T(8,128)(2,1)}), bf16[2,128,6144]{2,1,0:T(8,128)(2,1)}) %all-gather.8.cloned.1.call-update) | async-done | bytes 3145744 | tf_op jit(solution)/shard_map/all_gather | solution.py:30
  145.4 360.6 %while.14 = (s32[]{:T(128)}, f32[8,8,256,512]{3,2,1,0:T(8,128)}, s32[8]{0:T(128)S(1)}, s32[]{:T(128)}, bf16[256,6400]{1,0:T(8,128)(2,1)S(1)}, /*index=5*/bf16[51...) while((s32[]{:T(128)}, f32[8,8,256,512]{3,2,1,0:T(8,128)}, ...), condition=%wide.region_1.2_spmd, body=%wide.region_0.1_spmd.sunk | while | flops 12884901888 | bytes 85984392 | solution.py:25
  146.7 2.8 bitcast_dynamic-update-slice_fusion.18
  149.5 2.9 bitcast_dynamic-update-slice_fusion.19
  152.4 2.9 bitcast_dynamic-update-slice_fusion.20
  160.9 2.8 bitcast_dynamic-update-slice_fusion.23
  166.6 2.8 bitcast_dynamic-update-slice_fusion.25
  169.4 21.0 %bitcast_dynamic-update-slice_fusion.26 = f32[8,8,256,512]{3,2,1,0:T(8,128)} fusion(f32[8,8,256,512]{3,2,1,0:T(8,128)} %get-tuple-element.216, s32[]{:T(128)} %get-tuple-element.215, bf16[8,256,6144]{2,1,0:T(8,128)(2,1)} %bitcast_dynamic-update-slice_fusion.25, bf16[512,6144]{1,0:T(8,128)(2,1)} %get-tuple-element.245), kind=kOutput, calls=%fused_computation.2.clone.1 | convolution fusion | flops 12884901888 | bytes 35652096 | tf_op jit(solution)/shard_map/while/body/eval_jaxpr/kit,jt->kij/dot_general | solution.py:23
  191.8 2.8 bitcast_dynamic-update-slice_fusion.18
  194.6 2.9 bitcast_dynamic-update-slice_fusion.19
  197.5 2.9 bitcast_dynamic-update-slice_fusion.20
  206.0 2.8 bitcast_dynamic-update-slice_fusion.23
  211.7 2.8 bitcast_dynamic-update-slice_fusion.25
  214.5 21.1 %bitcast_dynamic-update-slice_fusion.26 = f32[8,8,256,512]{3,2,1,0:T(8,128)} fusion(f32[8,8,256,512]{3,2,1,0:T(8,128)} %get-tuple-element.216, s32[]{:T(128)} %get-tuple-element.215, bf16[8,256,6144]{2,1,0:T(8,128)(2,1)} %bitcast_dynamic-update-slice_fusion.25, bf16[512,6144]{1,0:T(8,128)(2,1)} %get-tuple-element.245), kind=kOutput, calls=%fused_computation.2.clone.1 | convolution fusion | flops 12884901888 | bytes 35652096 | tf_op jit(solution)/shard_map/while/body/eval_jaxpr/kit,jt->kij/dot_general | solution.py:23
  236.8 2.8 bitcast_dynamic-update-slice_fusion.18
  239.7 2.9 bitcast_dynamic-update-slice_fusion.19
  242.6 2.9 bitcast_dynamic-update-slice_fusion.20
  251.1 2.8 bitcast_dynamic-update-slice_fusion.23
  259.6 21.1 %bitcast_dynamic-update-slice_fusion.26 = f32[8,8,256,512]{3,2,1,0:T(8,128)} fusion(f32[8,8,256,512]{3,2,1,0:T(8,128)} %get-tuple-element.216, s32[]{:T(128)} %get-tuple-element.215, bf16[8,256,6144]{2,1,0:T(8,128)(2,1)} %bitcast_dynamic-update-slice_fusion.25, bf16[512,6144]{1,0:T(8,128)(2,1)} %get-tuple-element.245), kind=kOutput, calls=%fused_computation.2.clone.1 | convolution fusion | flops 12884901888 | bytes 35652096 | tf_op jit(solution)/shard_map/while/body/eval_jaxpr/kit,jt->kij/dot_general | solution.py:23
  281.9 2.8 bitcast_dynamic-update-slice_fusion.18
  284.8 2.9 bitcast_dynamic-update-slice_fusion.19
  287.6 2.9 bitcast_dynamic-update-slice_fusion.20
  296.2 2.8 bitcast_dynamic-update-slice_fusion.23
  304.7 21.1 %bitcast_dynamic-update-slice_fusion.26 = f32[8,8,256,512]{3,2,1,0:T(8,128)} fusion(f32[8,8,256,512]{3,2,1,0:T(8,128)} %get-tuple-element.216, s32[]{:T(128)} %get-tuple-element.215, bf16[8,256,6144]{2,1,0:T(8,128)(2,1)} %bitcast_dynamic-update-slice_fusion.25, bf16[512,6144]{1,0:T(8,128)(2,1)} %get-tuple-element.245), kind=kOutput, calls=%fused_computation.2.clone.1 | convolution fusion | flops 12884901888 | bytes 35652096 | tf_op jit(solution)/shard_map/while/body/eval_jaxpr/kit,jt->kij/dot_general | solution.py:23
  327.0 2.8 bitcast_dynamic-update-slice_fusion.18
  329.8 2.9 bitcast_dynamic-update-slice_fusion.19
  332.7 2.9 bitcast_dynamic-update-slice_fusion.20
  346.9 2.8 bitcast_dynamic-update-slice_fusion.25
  349.7 21.1 %bitcast_dynamic-update-slice_fusion.26 = f32[8,8,256,512]{3,2,1,0:T(8,128)} fusion(f32[8,8,256,512]{3,2,1,0:T(8,128)} %get-tuple-element.216, s32[]{:T(128)} %get-tuple-element.215, bf16[8,256,6144]{2,1,0:T(8,128)(2,1)} %bitcast_dynamic-update-slice_fusion.25, bf16[512,6144]{1,0:T(8,128)(2,1)} %get-tuple-element.245), kind=kOutput, calls=%fused_computation.2.clone.1 | convolution fusion | flops 12884901888 | bytes 35652096 | tf_op jit(solution)/shard_map/while/body/eval_jaxpr/kit,jt->kij/dot_general | solution.py:23
  372.1 2.8 bitcast_dynamic-update-slice_fusion.18
  374.9 2.9 bitcast_dynamic-update-slice_fusion.19
  377.8 2.9 bitcast_dynamic-update-slice_fusion.20
  392.0 2.8 bitcast_dynamic-update-slice_fusion.25
  394.8 21.1 %bitcast_dynamic-update-slice_fusion.26 = f32[8,8,256,512]{3,2,1,0:T(8,128)} fusion(f32[8,8,256,512]{3,2,1,0:T(8,128)} %get-tuple-element.216, s32[]{:T(128)} %get-tuple-element.215, bf16[8,256,6144]{2,1,0:T(8,128)(2,1)} %bitcast_dynamic-update-slice_fusion.25, bf16[512,6144]{1,0:T(8,128)(2,1)} %get-tuple-element.245), kind=kOutput, calls=%fused_computation.2.clone.1 | convolution fusion | flops 12884901888 | bytes 35652096 | tf_op jit(solution)/shard_map/while/body/eval_jaxpr/kit,jt->kij/dot_general | solution.py:23
  417.2 2.8 bitcast_dynamic-update-slice_fusion.18
  420.0 2.9 bitcast_dynamic-update-slice_fusion.19
  422.9 2.9 bitcast_dynamic-update-slice_fusion.20
  431.4 2.8 bitcast_dynamic-update-slice_fusion.23
  439.9 21.1 %bitcast_dynamic-update-slice_fusion.26 = f32[8,8,256,512]{3,2,1,0:T(8,128)} fusion(f32[8,8,256,512]{3,2,1,0:T(8,128)} %get-tuple-element.216, s32[]{:T(128)} %get-tuple-element.215, bf16[8,256,6144]{2,1,0:T(8,128)(2,1)} %bitcast_dynamic-update-slice_fusion.25, bf16[512,6144]{1,0:T(8,128)(2,1)} %get-tuple-element.245), kind=kOutput, calls=%fused_computation.2.clone.1 | convolution fusion | flops 12884901888 | bytes 35652096 | tf_op jit(solution)/shard_map/while/body/eval_jaxpr/kit,jt->kij/dot_general | solution.py:23
  462.2 2.8 bitcast_dynamic-update-slice_fusion.18
  465.1 2.9 bitcast_dynamic-update-slice_fusion.19
  467.9 2.9 bitcast_dynamic-update-slice_fusion.20
  476.5 2.8 bitcast_dynamic-update-slice_fusion.23
  485.0 21.1 %bitcast_dynamic-update-slice_fusion.26 = f32[8,8,256,512]{3,2,1,0:T(8,128)} fusion(f32[8,8,256,512]{3,2,1,0:T(8,128)} %get-tuple-element.216, s32[]{:T(128)} %get-tuple-element.215, bf16[8,256,6144]{2,1,0:T(8,128)(2,1)} %bitcast_dynamic-update-slice_fusion.25, bf16[512,6144]{1,0:T(8,128)(2,1)} %get-tuple-element.245), kind=kOutput, calls=%fused_computation.2.clone.1 | convolution fusion | flops 12884901888 | bytes 35652096 | tf_op jit(solution)/shard_map/while/body/eval_jaxpr/kit,jt->kij/dot_general | solution.py:23
  506.0 23.9 %broadcast_multiply_fusion = f32[8,8,256,512]{3,2,1,0:T(8,128)} fusion(f32[8,8,256,512]{3,2,1,0:T(8,128)} %get-tuple-element.140), kind=kLoop, calls=%fused_computation.11 | loop fusion | flops 8388608 | bytes 67108864 | tf_op jit(solution)/shard_map/mul | solution.py:54
  530.0 48.4 %mul.39 = f32[64,2,128,1,512]{4,3,2,1,0:T(1,128)} reshape(f32[8,8,256,512]{3,2,1,0:T(8,128)} %broadcast_multiply_fusion) | data formatting | bytes 67108864 | tf_op jit(solution)/shard_map/mul | solution.py:54
  (48 shorter events, 95.5 us)
Async XLA Ops:
  6.5 42.1 %all-gather.4.cloned.1.call-start = ((), (), s32[]{:S(2)}) async-start(), calls=%async_computation | async-start | bytes 1966080 | tf_op jit(solution)/shard_map/all_gather | solution.py:41
  7.3 88.2 %all-gather.6.cloned.1.call-start = ((), (), s32[]{:S(2)}) async-start(), calls=%async_computation.1 | async-start | bytes 7864320 | tf_op jit(solution)/shard_map/all_gather | solution.py:42
  48.7 94.6 %all-gather.8.cloned.1.call-start = ((), (), s32[]{:S(2)}) async-start(), calls=%async_computation.2 | async-start | bytes 4718592 | tf_op jit(solution)/shard_map/all_gather | solution.py:30
Sparse Core Ops, SparseCore 0:
  8.9 39.7 all-gather.3
  50.2 45.2 all-gather.5
  98.3 44.9 all-gather.7
where the time goes:
time: 586 us; the launch traced here: 585 us
  local copies, waits for them, and re-layouts  240 us (41%)
  matrix products  168 us (29%)
  waiting for transfers between devices  134 us (23%)
  other arithmetic  23.9 us (4%)
  between operations  13.1 us (2%)
    dot_general x8, matrix products, one_group(): jnp.einsum('kit,jt->kij', stacked, flat_cols, preferred_element_type=jnp....  168 us
    while x56, local copies, waits for them, and re-layouts  159 us
    mul x1, local copies, waits for them, and re-layouts, per_device(): return accumulated_sum * factor  48.4 us
    all_gather x1, waiting for transfers between devices, per_device(): columns = lax.all_gather(col_tiles, 'tm', axis=2, tiled=True)  46.7 us
    all_gather x1, waiting for transfers between devices, collect_rows(): return lax.all_gather(own_window, 'antb', axis=0, tiled=True)  45.1 us
    all_gather x1, waiting for transfers between devices, per_device(): col_tiles = lax.all_gather(samples, 'anta', axis=1, tiled=True)  41.4 us
    mul x1, other arithmetic, per_device(): return accumulated_sum * factor  23.9 us
    another operation x8, local copies, waits for them, and re-layouts, one_group(): stacked = jnp.stack(pieces, 0)  22.7 us
  transfers between devices with their start and end apart: 3, of which 3 were waited for; matrix products, arithmetic and copies ran while one was open for 0% of the time, Pallas kernels for 0%

commit v1 on v0

--- a/solution.py
+++ b/solution.py
@@ -38,7 +38,7 @@
     full_length = block_len * tm_size
     factor = 1.0 / math.sqrt(full_length)
     lag_start = lax.axis_index("tm") * lag_portion
-    col_tiles = lax.all_gather(samples, "anta", axis=1, tiled=True)
+    col_tiles = jnp.concatenate(lax.all_gather(samples, "anta"), axis=1)
     columns = lax.all_gather(col_tiles, "tm", axis=2, tiled=True)
     own_rows = lax.dynamic_slice_in_dim(
         columns, lax.axis_index("anta") * antenna_total, antenna_total, 1

time: 586 us -> 586 us (level)
  no operation moved by 1% of the time
where the time goes in v1:
time: 586 us; the launch traced here: 585 us
  local copies, waits for them, and re-layouts  240 us (41%)
  matrix products  168 us (29%)
  waiting for transfers between devices  134 us (23%)
  other arithmetic  23.9 us (4%)
  between operations  13.1 us (2%)
    dot_general x8, matrix products, one_group(): jnp.einsum('kit,jt->kij', stacked, flat_cols, preferred_element_type=jnp....  168 us
    while x56, local copies, waits for them, and re-layouts  159 us
    mul x1, local copies, waits for them, and re-layouts, per_device(): return accumulated_sum * factor  48.4 us
    all_gather x1, waiting for transfers between devices, per_device(): columns = lax.all_gather(col_tiles, 'tm', axis=2, tiled=True)  46.7 us
    all_gather x1, waiting for transfers between devices, collect_rows(): return lax.all_gather(own_window, 'antb', axis=0, tiled=True)  45.1 us
    all_gather x1, waiting for transfers between devices, per_device(): col_tiles = jnp.concatenate(lax.all_gather(samples, 'anta'), axis=1)  41.4 us
    mul x1, other arithmetic, per_device(): return accumulated_sum * factor  23.9 us
    another operation x8, local copies, waits for them, and re-layouts, one_group(): stacked = jnp.stack(pieces, 0)  22.7 us
  transfers between devices with their start and end apart: 3, of which 3 were waited for; matrix products, arithmetic and copies ran while one was open for 0% of the time, Pallas kernels for 0%

profile of v1, /device:TPU:0, one launch (start us, length us, event | category | flops | bytes accessed | tf_op | source)
XLA Modules:
  0.0 584.9 jit_solution(11511170079034413192)
XLA Ops:
  7.3 41.4 %all-gather.9.cloned.1.call-done = bf16[4,128,1536]{2,1,0:T(8,128)(2,1)} async-done(((bf16[1,128,1536]{2,1,0:T(8,128)(2,1)}), bf16[4,128,1536]{2,1,0:T(8,128)(2,1)}) %all-gather.9.cloned.1.call-update) | async-done | bytes 1572880 | tf_op jit(solution)/shard_map/all_gather | solution.py:41
  48.8 46.7 %all-gather.5.cloned.1.call-done = bf16[1,512,6144]{2,1,0:T(8,128)(2,1)} async-done(((bf16[1,512,1536]{2,1,0:T(8,128)(2,1)}), bf16[1,512,6144]{2,1,0:T(8,128)(2,1)}) %all-gather.5.cloned.1.call-update) | async-done | bytes 6291472 | tf_op jit(solution)/shard_map/all_gather | solution.py:42
  98.2 45.1 %all-gather.7.cloned.1.call-done = bf16[2,128,6144]{2,1,0:T(8,128)(2,1)} async-done(((bf16[1,128,6144]{2,1,0:T(8,128)(2,1)}), bf16[2,128,6144]{2,1,0:T(8,128)(2,1)}) %all-gather.7.cloned.1.call-update) | async-done | bytes 3145744 | tf_op jit(solution)/shard_map/all_gather | solution.py:30
  145.4 360.6 %while.14 = (s32[]{:T(128)}, f32[8,8,256,512]{3,2,1,0:T(8,128)}, s32[8]{0:T(128)S(1)}, s32[]{:T(128)}, bf16[256,6400]{1,0:T(8,128)(2,1)S(1)}, /*index=5*/bf16[51...) while((s32[]{:T(128)}, f32[8,8,256,512]{3,2,1,0:T(8,128)}, ...), condition=%wide.region_1.2_spmd, body=%wide.region_0.1_spmd.sunk | while | flops 12884901888 | bytes 85984392 | solution.py:25
  146.7 2.8 bitcast_dynamic-update-slice_fusion.18
  149.5 2.9 bitcast_dynamic-update-slice_fusion.19
  152.4 2.9 bitcast_dynamic-update-slice_fusion.20
  160.9 2.8 bitcast_dynamic-update-slice_fusion.23
  166.6 2.8 bitcast_dynamic-update-slice_fusion.25
  169.4 21.0 %bitcast_dynamic-update-slice_fusion.26 = f32[8,8,256,512]{3,2,1,0:T(8,128)} fusion(f32[8,8,256,512]{3,2,1,0:T(8,128)} %get-tuple-element.216, s32[]{:T(128)} %get-tuple-element.215, bf16[8,256,6144]{2,1,0:T(8,128)(2,1)} %bitcast_dynamic-update-slice_fusion.25, bf16[512,6144]{1,0:T(8,128)(2,1)} %get-tuple-element.245), kind=kOutput, calls=%fused_computation.2.clone.1 | convolution fusion | flops 12884901888 | bytes 35652096 | tf_op jit(solution)/shard_map/while/body/eval_jaxpr/kit,jt->kij/dot_general | solution.py:23
  191.8 2.8 bitcast_dynamic-update-slice_fusion.18
  194.6 2.9 bitcast_dynamic-update-slice_fusion.19
  197.5 2.9 bitcast_dynamic-update-slice_fusion.20
  206.0 2.8 bitcast_dynamic-update-slice_fusion.23
  211.7 2.8 bitcast_dynamic-update-slice_fusion.25
  214.5 21.1 %bitcast_dynamic-update-slice_fusion.26 = f32[8,8,256,512]{3,2,1,0:T(8,128)} fusion(f32[8,8,256,512]{3,2,1,0:T(8,128)} %get-tuple-element.216, s32[]{:T(128)} %get-tuple-element.215, bf16[8,256,6144]{2,1,0:T(8,128)(2,1)} %bitcast_dynamic-update-slice_fusion.25, bf16[512,6144]{1,0:T(8,128)(2,1)} %get-tuple-element.245), kind=kOutput, calls=%fused_computation.2.clone.1 | convolution fusion | flops 12884901888 | bytes 35652096 | tf_op jit(solution)/shard_map/while/body/eval_jaxpr/kit,jt->kij/dot_general | solution.py:23
  236.8 2.8 bitcast_dynamic-update-slice_fusion.18
  239.7 2.9 bitcast_dynamic-update-slice_fusion.19
  242.6 2.9 bitcast_dynamic-update-slice_fusion.20
  251.1 2.8 bitcast_dynamic-update-slice_fusion.23
  259.6 21.1 %bitcast_dynamic-update-slice_fusion.26 = f32[8,8,256,512]{3,2,1,0:T(8,128)} fusion(f32[8,8,256,512]{3,2,1,0:T(8,128)} %get-tuple-element.216, s32[]{:T(128)} %get-tuple-element.215, bf16[8,256,6144]{2,1,0:T(8,128)(2,1)} %bitcast_dynamic-update-slice_fusion.25, bf16[512,6144]{1,0:T(8,128)(2,1)} %get-tuple-element.245), kind=kOutput, calls=%fused_computation.2.clone.1 | convolution fusion | flops 12884901888 | bytes 35652096 | tf_op jit(solution)/shard_map/while/body/eval_jaxpr/kit,jt->kij/dot_general | solution.py:23
  281.9 2.8 bitcast_dynamic-update-slice_fusion.18
  284.8 2.9 bitcast_dynamic-update-slice_fusion.19
  287.6 2.9 bitcast_dynamic-update-slice_fusion.20
  296.2 2.8 bitcast_dynamic-update-slice_fusion.23
  304.7 21.1 %bitcast_dynamic-update-slice_fusion.26 = f32[8,8,256,512]{3,2,1,0:T(8,128)} fusion(f32[8,8,256,512]{3,2,1,0:T(8,128)} %get-tuple-element.216, s32[]{:T(128)} %get-tuple-element.215, bf16[8,256,6144]{2,1,0:T(8,128)(2,1)} %bitcast_dynamic-update-slice_fusion.25, bf16[512,6144]{1,0:T(8,128)(2,1)} %get-tuple-element.245), kind=kOutput, calls=%fused_computation.2.clone.1 | convolution fusion | flops 12884901888 | bytes 35652096 | tf_op jit(solution)/shard_map/while/body/eval_jaxpr/kit,jt->kij/dot_general | solution.py:23
  327.0 2.8 bitcast_dynamic-update-slice_fusion.18
  329.8 2.9 bitcast_dynamic-update-slice_fusion.19
  332.7 2.9 bitcast_dynamic-update-slice_fusion.20
  346.9 2.8 bitcast_dynamic-update-slice_fusion.25
  349.7 21.1 %bitcast_dynamic-update-slice_fusion.26 = f32[8,8,256,512]{3,2,1,0:T(8,128)} fusion(f32[8,8,256,512]{3,2,1,0:T(8,128)} %get-tuple-element.216, s32[]{:T(128)} %get-tuple-element.215, bf16[8,256,6144]{2,1,0:T(8,128)(2,1)} %bitcast_dynamic-update-slice_fusion.25, bf16[512,6144]{1,0:T(8,128)(2,1)} %get-tuple-element.245), kind=kOutput, calls=%fused_computation.2.clone.1 | convolution fusion | flops 12884901888 | bytes 35652096 | tf_op jit(solution)/shard_map/while/body/eval_jaxpr/kit,jt->kij/dot_general | solution.py:23
  372.1 2.8 bitcast_dynamic-update-slice_fusion.18
  374.9 2.9 bitcast_dynamic-update-slice_fusion.19
  377.8 2.9 bitcast_dynamic-update-slice_fusion.20
  392.0 2.8 bitcast_dynamic-update-slice_fusion.25
  394.8 21.1 %bitcast_dynamic-update-slice_fusion.26 = f32[8,8,256,512]{3,2,1,0:T(8,128)} fusion(f32[8,8,256,512]{3,2,1,0:T(8,128)} %get-tuple-element.216, s32[]{:T(128)} %get-tuple-element.215, bf16[8,256,6144]{2,1,0:T(8,128)(2,1)} %bitcast_dynamic-update-slice_fusion.25, bf16[512,6144]{1,0:T(8,128)(2,1)} %get-tuple-element.245), kind=kOutput, calls=%fused_computation.2.clone.1 | convolution fusion | flops 12884901888 | bytes 35652096 | tf_op jit(solution)/shard_map/while/body/eval_jaxpr/kit,jt->kij/dot_general | solution.py:23
  417.2 2.8 bitcast_dynamic-update-slice_fusion.18
  420.0 2.9 bitcast_dynamic-update-slice_fusion.19
  422.9 2.9 bitcast_dynamic-update-slice_fusion.20
  431.4 2.8 bitcast_dynamic-update-slice_fusion.23
  439.9 21.1 %bitcast_dynamic-update-slice_fusion.26 = f32[8,8,256,512]{3,2,1,0:T(8,128)} fusion(f32[8,8,256,512]{3,2,1,0:T(8,128)} %get-tuple-element.216, s32[]{:T(128)} %get-tuple-element.215, bf16[8,256,6144]{2,1,0:T(8,128)(2,1)} %bitcast_dynamic-update-slice_fusion.25, bf16[512,6144]{1,0:T(8,128)(2,1)} %get-tuple-element.245), kind=kOutput, calls=%fused_computation.2.clone.1 | convolution fusion | flops 12884901888 | bytes 35652096 | tf_op jit(solution)/shard_map/while/body/eval_jaxpr/kit,jt->kij/dot_general | solution.py:23
  462.2 2.8 bitcast_dynamic-update-slice_fusion.18
  465.1 2.9 bitcast_dynamic-update-slice_fusion.19
  467.9 2.9 bitcast_dynamic-update-slice_fusion.20
  476.5 2.8 bitcast_dynamic-update-slice_fusion.23
  485.0 21.1 %bitcast_dynamic-update-slice_fusion.26 = f32[8,8,256,512]{3,2,1,0:T(8,128)} fusion(f32[8,8,256,512]{3,2,1,0:T(8,128)} %get-tuple-element.216, s32[]{:T(128)} %get-tuple-element.215, bf16[8,256,6144]{2,1,0:T(8,128)(2,1)} %bitcast_dynamic-update-slice_fusion.25, bf16[512,6144]{1,0:T(8,128)(2,1)} %get-tuple-element.245), kind=kOutput, calls=%fused_computation.2.clone.1 | convolution fusion | flops 12884901888 | bytes 35652096 | tf_op jit(solution)/shard_map/while/body/eval_jaxpr/kit,jt->kij/dot_general | solution.py:23
  506.0 23.9 %broadcast_multiply_fusion = f32[8,8,256,512]{3,2,1,0:T(8,128)} fusion(f32[8,8,256,512]{3,2,1,0:T(8,128)} %get-tuple-element.140), kind=kLoop, calls=%fused_computation.11 | loop fusion | flops 8388608 | bytes 67108864 | tf_op jit(solution)/shard_map/mul | solution.py:54
  530.0 48.4 %mul.39 = f32[64,2,128,1,512]{4,3,2,1,0:T(1,128)} reshape(f32[8,8,256,512]{3,2,1,0:T(8,128)} %broadcast_multiply_fusion) | data formatting | bytes 67108864 | tf_op jit(solution)/shard_map/mul | solution.py:54
  (48 shorter events, 95.5 us)
Async XLA Ops:
  6.5 42.1 %all-gather.9.cloned.1.call-start = ((), (), s32[]{:S(2)}) async-start(), calls=%async_computation.2 | async-start | bytes 1966080 | tf_op jit(solution)/shard_map/all_gather | solution.py:41
  7.3 88.2 %all-gather.5.cloned.1.call-start = ((), (), s32[]{:S(2)}) async-start(), calls=%async_computation | async-start | bytes 7864320 | tf_op jit(solution)/shard_map/all_gather | solution.py:42
  48.7 94.6 %all-gather.7.cloned.1.call-start = ((), (), s32[]{:S(2)}) async-start(), calls=%async_computation.1 | async-start | bytes 4718592 | tf_op jit(solution)/shard_map/all_gather | solution.py:30
Sparse Core Ops, SparseCore 0:
  8.9 39.7 all-gather.8
  50.2 45.2 all-gather.4
  98.3 44.9 all-gather.6
